TPU v7x, 32 devices: a whole 2x2x4 slice. The times are simulated.
32 devices in a mesh: row: 4 (over y, x), col: 2 (over core), layer: 4 (over z).
Axes of the slice: x: 2, y: 2, z: 4, core: 2. Of those that a mesh axis runs over, the one named last changes fastest.
Arguments:
- design: float32 [1024, 8192], P(('row', 'layer'), 'col'), may hold values from -6 to 6
- responses: float32 [1024, 8192], P(('row', 'layer'), 'col'), may hold values from -0.1875 to 0.1875
Outputs:
- normal_update: float32 [8192, 8192], P('row', ('col', 'layer'))
All inputs are finite; a program needn't handle non-finite values.
Results may differ from a plain program's by a relative error of at most 0.00008.
Values sent between devices are 32-bit elements; how exact they have to be, the bound alone decides.
No kernel may reach another device: no remote copies, remote signals or barrier semaphores. Data moves between devices by JAX's collectives and lax.ppermute only.
A program may use at most 128 MiB of HBM per device.

v0:
```python
import jax
import jax.numpy as jnp
from jax import lax
from jax.sharding import PartitionSpec as P

HIGHEST = lax.Precision.HIGHEST


def body(design, responses):
    widened = lax.all_gather(design, "col", axis=1, tiled=True)
    design_panel = lax.all_to_all(widened, "row", split_axis=1, concat_axis=0, tiled=True)
    partial_value = lax.dot_general(
        design_panel,
        lax.all_gather(responses, "row", axis=0, tiled=True),
        (((0,), (0,)), ((), ())),
        precision=HIGHEST,
        preferred_element_type=jnp.float32,
    )
    result = lax.psum_scatter(partial_value, "layer", scatter_dimension=1, tiled=True)
    return result


def solution(mesh):
    return jax.shard_map(
        body,
        mesh=mesh,
        in_specs=(P(("row", "layer"), "col"), P(("row", "layer"), "col")),
        out_specs=P("row", ("col", "layer")),
        check_vma=False,
    )
```

profile of v0, /device:TPU:0, one launch (start us, length us, event | category | flops | bytes accessed | tf_op | source)
XLA Modules:
  0.0 685.0 jit_solution(15478034845018122340)
XLA Ops:
  6.5 0.0 all-gather.3.cloned.1.call-start
  6.5 0.7 all-gather.3.cloned.1.call-update
  7.3 0.0 all-gather.5.cloned.1.call-start
  7.3 0.7 all-gather.5.cloned.1.call-update
  8.0 0.0 reduce-scatter.2.cloned.1.call-start
  8.1 14.2 %all-gather.3.cloned.1.call-done = f32[64,8192]{1,0:T(8,128)} async-done(((f32[64,4096]{1,0:T(8,128)}), f32[64,8192]{1,0:T(8,128)}) %all-gather.3.cloned.1.call-update) | async-done | bytes 2097168 | tf_op jit(solution)/shard_map/all_gather | solution.py:10
  22.2 1.7 copy.7
  23.9 40.8 %all_to_all.19 = f32[64,4,2048]{2,0,1:T(8,128)S(1)} all-to-all(f32[64,4,2048]{2,0,1:T(8,128)S(1)} %bitcast.10), channel_id=1, replica_groups=mesh['row'=4,'col'=2,'layer'=4] {'row'}, dimensions={1} | all-to-all | bytes 4194304 | tf_op jit(solution)/shard_map/all_to_all | solution.py:11
  64.7 29.8 %all-gather.5.cloned.1.call-done = f32[256,4096]{1,0:T(8,128)} async-done(((f32[64,4096]{1,0:T(8,128)}), f32[256,4096]{1,0:T(8,128)}) %all-gather.5.cloned.1.call-update) | async-done | bytes 4194320 | tf_op jit(solution)/shard_map/all_gather | solution.py:14
  94.5 31.5 %fusion = f32[2048,4096]{1,0:T(8,128)} fusion(f32[256,2048]{1,0:T(8,128)S(1)} %bitcast.9, f32[256,4096]{1,0:T(8,128)} %all-gather.5.cloned.1.call-done), kind=kOutput, calls=%fused_computation.1 | convolution fusion | flops 25769803776 | bytes 39845888 | tf_op jit(solution)/shard_map/dot_general | solution.py:12
  126.1 0.0 reduce-scatter.2.cloned.1.call-update
  126.1 552.3 %reduce-scatter.2.cloned.1.call-done = f32[2048,1024]{1,0:T(8,128)} async-done(((f32[2048,4096]{1,0:T(8,128)}), f32[2048,1024]{1,0:T(8,128)}) %reduce-scatter.2.cloned.1.call-update) | async-done | bytes 8388624 | tf_op jit(solution)/shard_map/reduce_scatter | solution.py:19
Async XLA Ops:
  6.5 15.7 %all-gather.3.cloned.1.call-start = ((), (), s32[]{:S(2)}) async-start(), calls=%async_computation.2 | async-start | bytes 3145728 | tf_op jit(solution)/shard_map/all_gather | solution.py:10
  7.3 87.3 %all-gather.5.cloned.1.call-start = ((), (), s32[]{:S(2)}) async-start(), calls=%async_computation.3 | async-start | bytes 5242880 | tf_op jit(solution)/shard_map/all_gather | solution.py:14
  8.0 670.4 %reduce-scatter.2.cloned.1.call-start = ((), (), s32[]{:S(2)}) async-start(), calls=%async_computation.4 | async-start | bytes 41943040 | tf_op jit(solution)/shard_map/reduce_scatter | solution.py:19
Sparse Core Ops, SparseCore 0:
  8.9 13.2 all-gather.2
  24.0 70.4 all-gather.4
  126.2 552.1 reduce-scatter.1
where the time goes:
time: 685 us
  waiting for transfers between devices  598 us (87%)
  blocking collectives  40.8 us (6%)
  matrix products  31.5 us (5%)
  between operations  13.1 us (2%)
    reduce_scatter x1, waiting for transfers between devices, body(): lax.psum_scatter(partial_value, 'layer', scatter_dimension=1, tiled=True)  552 us
    all_to_all x1, blocking collectives, body(): lax.all_to_all(widened, 'row', split_axis=1, concat_axis=0, tiled=True)  40.8 us
    dot_general x1, matrix products, body(): lax.dot_general(design_panel, lax.all_gather(responses, 'row', axis=0, ti...  31.5 us
    all_gather x1, waiting for transfers between devices, body(): lax.all_gather(responses, 'row', axis=0, tiled=True)  29.8 us
    all_gather x1, waiting for transfers between devices, body(): widened = lax.all_gather(design, 'col', axis=1, tiled=True)  14.2 us
  transfers between devices with their start and end apart: 3, of which 3 were waited for; matrix products, arithmetic and copies ran while one was open for 0% of the time, Pallas kernels for 0%

commit v1 on v0

v1 whole, which is shorter than its diff:
```python
import functools

import jax
import jax.numpy as jnp
from jax import lax
from jax.experimental import pallas as pl
from jax.experimental.pallas import tpu as pltpu
from jax.sharding import PartitionSpec as P


FINAL = 512
HIGHEST = lax.Precision.HIGHEST
T0 = (((0,), (0,)), ((), ()))


def split(x):
    hi = x.astype(jnp.bfloat16)
    return hi, (x - hi.astype(jnp.float32)).astype(jnp.bfloat16)


def update_kernel(counts, spans, tiles, sides, has_acc, final, flags_ref, *refs):
    refs = list(refs)
    groups = [[refs.pop(0) for _ in range(count)] for count in counts]
    resp = [refs.pop(0) for _ in spans]
    acc_ref = refs.pop(0) if has_acc else None
    out_ref, held = refs[-2:]
    step = pl.program_id(0)
    depth = held.shape[0] // 3
    size = groups[0][0].shape[1] // tiles

    @pl.when(step == 0)
    def _():
        hi, lo = split(jnp.concatenate([p[start : start + rows, :] for p, (start, rows) in zip(resp, spans)], axis=0))
        held[:depth, :] = hi
        held[depth : 2 * depth, :] = lo
        held[2 * depth :, :] = hi

    def tile(pieces, at):
        at = pl.ds(pl.multiple_of(at * size, size), size)
        blocks = [p[:, at] for p in pieces]
        if final:
            blocks = [jnp.where(flags_ref[1] == 1, *blocks)]
        hi, lo = split(jnp.concatenate(blocks, axis=0))
        total = lax.dot_general(jnp.concatenate([hi, hi, lo], axis=0), held[...], T0, preferred_element_type=jnp.float32)
        if has_acc:
            total += acc_ref[pl.ds(pl.multiple_of((sides[0] * tiles + step) * size, size), size), :]
        if final:
            out_ref[...] = total
        else:
            out_ref[pl.ds(pl.multiple_of(step * size, size), size), :] = total

    for i, pieces in enumerate(groups):
        pl.when((step >= i * tiles) & (step < (i + 1) * tiles))(lambda i=i, pieces=pieces: tile(pieces, step - i * tiles))


def update(flags, groups, resp, acc, size, sides=(0, 1), final=False, base=None):
    half, width = groups[0][0].shape[1], resp[0][0].shape[1]
    arrays, spans = [r[0] for r in resp], [r[1:] for r in resp]
    depth = sum(rows for _, rows in spans)
    tiles = half // size
    has_acc, has_base = acc is not None, base is not None
    whole = pl.BlockSpec(memory_space=pltpu.VMEM)
    flip = sides[0]
    placed = pl.BlockSpec((size, width), lambda i, flags: ((flip + flags[0] - 2 * flip * flags[0]) * tiles + i, 0))
    shape = (2 * half, width)
    operands = [x for group in groups for x in group] + arrays + ([acc] if has_acc else [])
    return pl.pallas_call(
        functools.partial(update_kernel, [len(g) for g in groups], spans, tiles, sides, has_acc, final),
        out_shape=jax.ShapeDtypeStruct(shape, jnp.float32) if final else pltpu.VMEM(shape, jnp.float32),
        grid_spec=pltpu.PrefetchScalarGridSpec(
            num_scalar_prefetch=1,
            grid=(len(sides) * tiles,),
            in_specs=[whole] * len(operands) + [pl.BlockSpec(memory_space=pl.ANY)] * has_base,
            out_specs=placed if final else whole,
            scratch_shapes=[pltpu.VMEM((3 * depth, width), jnp.bfloat16)],
        ),
        input_output_aliases={1 + len(operands): 0} if has_base else {len(operands): 0} if has_acc and not final else {},
        compiler_params=pltpu.CompilerParams(vmem_limit_bytes=12 << 20),
        cost_estimate=pl.CostEstimate(
            flops=6 * depth * len(sides) * half * width,
            bytes_accessed=4 * (depth * (2 * half + width) + (1 + has_acc) * len(sides) * half * width),
            transcendentals=0,
        ),
    )(flags, *operands, *([base] if has_base else []))


def by_permutes(sizes, design, responses):
    layers = sizes["layer"]
    last = layers - 1
    row, core, layer = lax.axis_index("row"), lax.axis_index("col"), lax.axis_index("layer")
    rows, half = design.shape[0], design.shape[1] // 4
    width = responses.shape[1] // layers

    swap = lambda x: lax.ppermute(x, "col", [(0, 1), (1, 0)])
    over_row = lambda x, m: lax.ppermute(x, "row", [(i, i ^ m) for i in range(sizes["row"])])
    along = lambda x, pairs: lax.ppermute(x, "layer", pairs)

    columns = lambda d: lax.dynamic_slice(responses, (0, ((layer - d) % layers) * width), (rows, width))
    z = [columns(0)] + [along(columns(d), [((i + d) % layers, i) for i in range(layers)]) for d in (1, 2, 3)]
    r0 = [z[0]] + [over_row(z[0], m) for m in (1, 2, 3)]
    far = jnp.concatenate([jnp.where(layer == last, z[3], z[1]), z[2], jnp.where(layer == last, z[1], z[3])], axis=0)
    r = [far] + [over_row(far, m) for m in (1, 2, 3)]

    piece = lambda at, h: lax.dynamic_slice(design, (0, (2 * at + h) * half), (rows, half))
    got = [swap(piece(at, 1 - core)) for at in (0, 1)]
    mine = []
    for m in range(4):
        to = row ^ m
        sent = jnp.where(to // 2 == core, piece(to % 2, core), jnp.where(to % 2 == 0, got[0], got[1]))
        mine.append(over_row(sent, m) if m else sent)
    outer = (layer == 0) | (layer == last)
    a = {0: [jnp.concatenate(mine[:2], axis=0), jnp.concatenate(mine[2:], axis=0)], 1: [], 2: [], 3: []}
    for h in (0, 1):
        left = along(a[0][h], [(1, 0), (2, 1), (3, 2)])
        right = along(a[0][h], [(0, 1), (1, 2), (2, 3)])
        a[1].append(jnp.where(layer == last, right, left))
        left2 = along(left, [(1, 0), (2, 1)])
        right2 = along(right, [(1, 2), (2, 3)])
        a[2].append(jnp.where(layer < 2, left2, right2))
        ends = along(a[2][h], [(1, 0), (2, 3)])
        if h == 0:
            ends, right = lax.optimization_barrier((ends, right))
            a[3].append(jnp.where(outer, ends, right))
    b = {slot: [swap(x) for x in a[slot]] for slot in range(4)}

    def resp(slot, halves):
        ms = [m for h in halves for m in (2 * h, 2 * h + 1)]
        return [(r[m], (slot - 1) * rows, rows) if slot else (r0[m], 0, rows) for m in ms]

    flags = jnp.stack([core, outer.astype(core.dtype)])
    total = None
    for slot, halves in ((0, (0, 1)), (1, (0, 1)), (2, (0, 1)), (3, (0,))):
        total = update(flags, [[a[slot][h] for h in halves], [b[slot][h] for h in halves]], resp(slot, halves), total, 512)
    swapped = [swap(ends), swap(right)]
    out = None
    for side, pieces in ((0, [ends, right]), (1, swapped)):
        out = update(flags, [pieces], resp(3, (1,)), total, FINAL, sides=(side,), final=True, base=out)
    return out


def by_collectives(sizes, design, responses):
    rows, layers = sizes["row"], sizes["layer"]
    widened = lax.all_gather(design, "col", axis=1, tiled=True)
    panel = lax.all_to_all(widened, "row", split_axis=1, concat_axis=0, tiled=True)
    panel = lax.all_gather(panel, "layer", axis=0, tiled=True)
    block = lax.all_to_all(responses, "layer", split_axis=1, concat_axis=0, tiled=True)
    block = lax.all_gather(block, "row", axis=0, tiled=True)
    block = block.reshape(rows, layers, -1, block.shape[1]).swapaxes(0, 1).reshape(block.shape)
    return lax.dot_general(panel, block, T0, precision=HIGHEST, preferred_element_type=jnp.float32)


def solution(mesh):
    sizes = dict(mesh.shape)
    small = (sizes["row"], sizes["col"], sizes["layer"]) == (4, 2, 4)
    plan = by_permutes if small else by_collectives

    def body(design, responses):
        return plan(sizes, design, responses)

    return jax.shard_map(
        body,
        mesh=mesh,
        in_specs=(P(("row", "layer"), "col"), P(("row", "layer"), "col")),
        out_specs=P("row", ("col", "layer")),
        check_vma=False,
    )
```

time: 685 us -> 145 us (0.21)
  waiting for transfers between devices: 598 us -> 65.7 us
  starting transfers between devices: 0.08 us -> 44.1 us
  blocking collectives: 40.8 us -> 0 us
  matrix products: 31.5 us -> 0 us
  Pallas kernels: 0 us -> 27.5 us
  between operations: 13.1 us -> 0.29 us
    reduce_scatter x1 -> x0, waiting for transfers between devices: 552 us -> none  [body(): lax.psum_scatter(partial_value, 'layer', scatter_dimension=1, tiled=True)]
    ppermute x0 -> x33, waiting for transfers between devices: none -> 65.7 us  [the longest x13 45 us: by_permutes(): along = lambda x, pairs: lax.ppermute(x, 'layer', pairs)]
    ppermute x0 -> x33, starting transfers between devices: none -> 44.1 us  [the longest x13 31 us: by_permutes(): along = lambda x, pairs: lax.ppermute(x, 'layer', pairs)]
    all_gather x2 -> x0, waiting for transfers between devices: 43.9 us -> none  [the longest x1 29.8 us: body(): lax.all_gather(responses, 'row', axis=0, tiled=True)]
    all_to_all x1 -> x0, blocking collectives: 40.8 us -> none  [body(): lax.all_to_all(widened, 'row', split_axis=1, concat_axis=0, tiled=True)]
    dot_general x1 -> x0, matrix products: 31.5 us -> none  [body(): lax.dot_general(design_panel, lax.all_gather(responses, 'row', axis=0, ti...]
    pallas_call x0 -> x6, Pallas kernels: none -> 27.5 us  [update(): pl.pallas_call(functools.partial(update_kernel, [len(g) for g in groups],...]
  transfers between devices with their start and end apart: 3 -> 33, of which waited for: 3 -> 15; matrix products, arithmetic and copies ran while one was open for 0% -> 3% of each run, Pallas kernels for 0% -> 17%
where the time goes in v1:
time: 145 us; the launch traced here: 144 us
  waiting for transfers between devices  65.7 us (45%)
  starting transfers between devices  44.1 us (30%)
  Pallas kernels  27.5 us (19%)
  other arithmetic  3.84 us (3%)
  local copies, waits for them, and re-layouts  3.11 us (2%)
    ppermute x13, waiting for transfers between devices, by_permutes(): along = lambda x, pairs: lax.ppermute(x, 'layer', pairs)  45 us
    ppermute x13, starting transfers between devices, by_permutes(): along = lambda x, pairs: lax.ppermute(x, 'layer', pairs)  31 us
    pallas_call x6, Pallas kernels, update(): pl.pallas_call(functools.partial(update_kernel, [len(g) for g in groups],...  27.5 us
    ppermute x9, waiting for transfers between devices, by_permutes(): lax.ppermute(x, 'row', [(i, i ^ m) for i in range(sizes['row'])])  19.1 us
    ppermute x9, starting transfers between devices, by_permutes(): lax.ppermute(x, 'row', [(i, i ^ m) for i in range(sizes['row'])])  10.7 us
  transfers between devices with their start and end apart: 33, of which 15 were waited for; matrix products, arithmetic and copies ran while one was open for 3% of the time, Pallas kernels for 17%

profile of v1, /device:TPU:0, one launch (start us, length us, event | category | flops | bytes accessed | tf_op | source)
XLA Modules:
  0.0 144.5 jit_solution(10632513039399960943)
XLA Ops:
  0.0 1.1 constant_dynamic-slice_fusion.4
  1.1 0.6 collective-permute-start.1
  1.7 1.1 collective-permute-done.1
  3.2 1.3 select_select_fusion.1
  4.5 2.9 %collective-permute-start.16 = (f32[64,1024]{1,0:T(8,128)S(1)}, f32[64,1024]{1,0:T(8,128)S(1)}, u32[]{:S(2)}, u32[]{:S(2)}) collective-permute-start(f32[64,1024]{1,0:T(8,128)S(1)} %get-tuple-element.10), channel_id=1, source_target_pairs={{0,8},{8,0},{16,24},{24,16},{1,9},{9,1},{17,25},{25,17},{2,10},{10... | collective-permute-start | bytes 786440 | tf_op jit(solution)/shard_map/ppermute | solution.py:95
  7.4 1.5 %collective-permute-start.3 = (f32[64,1024]{1,0:T(8,128)S(1)}, f32[64,1024]{1,0:T(8,128)S(1)}, u32[]{:S(2)}, u32[]{:S(2)}) collective-permute-start(f32[64,1024]{1,0:T(8,128)S(1)} %get-tuple-element.11), channel_id=1, source_target_pairs={{0,24},{8,16},{16,8},{24,0},{1,25},{9,17},{17,9},{25,1},{2,26},{10... | collective-permute-start | bytes 786440 | tf_op jit(solution)/shard_map/ppermute | solution.py:95
  9.0 5.5 %collective-permute-done.16 = f32[64,1024]{1,0:T(8,128)S(1)} collective-permute-done((f32[64,1024]{1,0:T(8,128)S(1)}, f32[64,1024]{1,0:T(8,128)S(1)}, u32[]{:S(2)}, u32[]{:S(2)}) %collective-permute-start.16) | collective-permute-done | bytes 262176 | tf_op jit(solution)/shard_map/ppermute | solution.py:95
  14.6 4.0 %collective-permute-start.19 = (f32[128,1024]{1,0:T(8,128)S(1)}, f32[128,1024]{1,0:T(8,128)S(1)}, u32[]{:S(2)}, u32[]{:S(2)}) collective-permute-start(f32[128,1024]{1,0:T(8,128)S(1)} %pad_maximum_fusion.1.refs_0_), channel_id=1, source_target_pairs={{0,1},{1,2},{2,3},{4,5},{5,6},{6,7},{8,9},{9,10},{10,11},{12,13},{... | collective-permute-start | bytes 1572872 | tf_op jit(solution)/shard_map/ppermute | solution.py:96
  18.7 1.3 collective-permute-start.17
  20.0 2.0 %constant_dynamic-slice_fusion = (f32[64,1024]{1,0:T(8,128)S(1)}, f32[64,1024]{1,0:T(8,128)S(1)}, f32[64,1024]{1,0:T(8,128)S(1)}, f32[64,1024]{1,0:T(8,128)}) fusion(f32[64,4096]{1,0:T(8,128)} %param.3, s32[]{:T(128)S(6)} %select_n.222, s32[]{:T(128)S(6)} %select_n.196, s32[]{:T(128)S(6)} %select_n.194, s32[]{:T(128)S(6)} %select_n.199), kind=kLoop, calls=%fused_computation.15 | loop fusion | bytes 2097168 | tf_op jit(solution)/shard_map/dynamic_slice | solution.py:98
  22.0 4.7 %collective-permute-start.12 = (f32[64,1024]{1,0:T(8,128)S(1)}, f32[64,1024]{1,0:T(8,128)}, u32[]{:S(2)}, u32[]{:S(2)}) collective-permute-start(f32[64,1024]{1,0:T(8,128)S(1)} %get-tuple-element.14), channel_id=1, source_target_pairs={{1,0},{2,1},{3,2},{0,3},{5,4},{6,5},{7,6},{4,7},{9,8},{10,9},{11,1... | collective-permute-start | bytes 786440 | tf_op jit(solution)/shard_map/ppermute | solution.py:96
  26.6 1.0 collective-permute-start.13
  27.7 15.0 %collective-permute-done.12 = f32[64,1024]{1,0:T(8,128)} collective-permute-done((f32[64,1024]{1,0:T(8,128)S(1)}, f32[64,1024]{1,0:T(8,128)}, u32[]{:S(2)}, u32[]{:S(2)}) %collective-permute-start.12) | collective-permute-done | bytes 262176 | tf_op jit(solution)/shard_map/ppermute | solution.py:96
  42.7 12.0 %collective-permute-start.6 = (f32[128,1024]{1,0:T(8,128)S(1)}, f32[128,1024]{1,0:T(8,128)S(1)}, u32[]{:S(2)}, u32[]{:S(2)}) collective-permute-start(f32[128,1024]{1,0:T(8,128)S(1)} %constant_dynamic-update-slice_fusion.refs_1_), channel_id=1, source_target_pairs={{0,1},{1,2},{2,3},{4,5},{5,6},{6,7},{8,9},{9,10},{10,11},{12,13},{... | collective-permute-start | bytes 1572872 | tf_op jit(solution)/shard_map/ppermute | solution.py:96
  54.7 1.3 collective-permute-start.4
  56.1 2.8 %collective-permute-done.13 = f32[64,1024]{1,0:T(8,128)} collective-permute-done((f32[64,1024]{1,0:T(8,128)}, f32[64,1024]{1,0:T(8,128)}, u32[]{:S(2)}, u32[]{:S(2)}) %collective-permute-start.13) | collective-permute-done | bytes 262176 | tf_op jit(solution)/shard_map/ppermute | solution.py:96
  58.9 2.5 %collective-permute-start.32 = (f32[64,1024]{1,0:T(8,128)S(1)}, f32[64,1024]{1,0:T(8,128)S(1)}, u32[]{:S(2)}, u32[]{:S(2)}) collective-permute-start(f32[64,1024]{1,0:T(8,128)S(1)} %get-tuple-element.13.refs_4_), channel_id=1, source_target_pairs={{0,24},{8,16},{16,8},{24,0},{1,25},{9,17},{17,9},{25,1},{2,26},{10... | collective-permute-start | bytes 786440 | tf_op jit(solution)/shard_map/ppermute | solution.py:95
  61.4 0.7 collective-permute-start.20
  62.1 1.3 collective-permute-start.18
  63.4 1.1 broadcast_select_fusion.6
  64.4 1.0 pad_maximum_fusion.refs_4_.refs_2_
  65.5 0.7 collective-permute-done.32.refs_7_
  66.7 4.3 %collective-permute-done.4 = f32[128,1024]{1,0:T(8,128)S(1)} collective-permute-done((f32[128,1024]{1,0:T(8,128)S(1)}, f32[128,1024]{1,0:T(8,128)S(1)}, u32[]{:S(2)}, u32[]{:S(2)}) %collective-permute-start.4) | collective-permute-done | bytes 524320 | tf_op jit(solution)/shard_map/ppermute | solution.py:96
  71.0 0.7 collective-permute-start.7
  71.8 0.6 collective-permute-start.31
  72.4 4.2 %collective-permute-done.18 = f32[128,1024]{1,0:T(8,128)S(1)} collective-permute-done((f32[128,1024]{1,0:T(8,128)S(1)}, f32[128,1024]{1,0:T(8,128)S(1)}, u32[]{:S(2)}, u32[]{:S(2)}) %collective-permute-start.18) | collective-permute-done | bytes 524320 | tf_op jit(solution)/shard_map/ppermute | solution.py:96
  76.6 0.5 collective-permute-start.30
  77.2 1.0 collective-permute-done.31.refs_6_
  78.2 0.6 collective-permute-start.23
  78.8 7.0 %collective-permute-done.30.refs_5_ = f32[64,1024]{1,0:T(8,128)S(1)} collective-permute-done((f32[64,1024]{1,0:T(8,128)S(1)}, f32[64,1024]{1,0:T(8,128)S(1)}, u32[]{:S(2)}, u32[]{:S(2)}) %collective-permute-start.30) | collective-permute-done | bytes 262176 | tf_op jit(solution)/shard_map/ppermute | solution.py:95
  85.8 1.0 collective-permute-start.15
  86.8 1.0 collective-permute-start.14
  87.8 1.3 collective-permute-start.5
  89.1 1.3 collective-permute-start.21
  90.5 4.9 %shard_map.28.refs_8_ = f32[2048,1024]{1,0:T(8,128)S(1)} custom-call(s32[2]{0:T(128)S(1)} %pad_add_fusion.flags_ref, f32[128,1024]{1,0:T(8,128)S(1)} %pad_maximum_fusion.1.refs_0_, f32[128,1024]{1,0:T(8,128)S(1)} %constant_dynamic-update-slice_fusion.refs_1_, f32[128,1024]{1,0:T(8,128)S(1)} %collective-permute-done.28.refs_2_, ...), custom_call_target="tpu_custom_call" | custom-call | flops 3221225472 | bytes 11534336 | tf_op jit(solution)/shard_map/pallas_call | solution.py:67
  95.4 7.4 %collective-permute-done.5 = f32[128,1024]{1,0:T(8,128)S(1)} collective-permute-done((f32[128,1024]{1,0:T(8,128)S(1)}, f32[128,1024]{1,0:T(8,128)S(1)}, u32[]{:S(2)}, u32[]{:S(2)}) %collective-permute-start.5) | collective-permute-done | bytes 524320 | tf_op jit(solution)/shard_map/ppermute | solution.py:96
  102.8 5.6 %collective-permute-done.21 = f32[128,1024]{1,0:T(8,128)S(1)} collective-permute-done((f32[128,1024]{1,0:T(8,128)S(1)}, f32[128,1024]{1,0:T(8,128)S(1)}, u32[]{:S(2)}, u32[]{:S(2)}) %collective-permute-start.21) | collective-permute-done | bytes 524320 | tf_op jit(solution)/shard_map/ppermute | solution.py:96
  108.5 0.6 collective-permute-start.25
  109.0 4.2 %collective-permute-done.15.refs_7_.refs_3_ = f32[192,1024]{1,0:T(8,128)S(1)} collective-permute-done((f32[192,1024]{1,0:T(8,128)S(1)}, f32[192,1024]{1,0:T(8,128)S(1)}, u32[]{:S(2)}, u32[]{:S(2)}) %collective-permute-start.15) | collective-permute-done | bytes 786464 | tf_op jit(solution)/shard_map/ppermute | solution.py:95
  113.2 1.5 %collective-permute-start.8 = (f32[128,1024]{1,0:T(8,128)S(1)}, f32[128,1024]{1,0:T(8,128)S(1)}, u32[]{:S(2)}, u32[]{:S(2)}) collective-permute-start(f32[128,1024]{1,0:T(8,128)S(1)} %broadcast_select_fusion.4.refs_1_), channel_id=1, source_target_pairs={{1,0},{2,3},{5,4},{6,7},{9,8},{10,11},{13,12},{14,15},{17,16},{18,... | collective-permute-start | bytes 1572872 | tf_op jit(solution)/shard_map/ppermute | solution.py:96
  114.7 0.7 collective-permute-done.14.refs_6_.refs_2_
  115.5 0.6 collective-permute-start.10
  116.2 5.6 %shard_map.29.refs_8_ = f32[2048,1024]{1,0:T(8,128)S(1)} custom-call(s32[2]{0:T(128)S(1)} %pad_add_fusion.flags_ref, f32[128,1024]{1,0:T(8,128)S(1)} %broadcast_select_fusion.1.refs_0_, f32[128,1024]{1,0:T(8,128)S(1)} %broadcast_select_fusion.refs_1_, f32[128,1024]{1,0:T(8,128)S(1)} %collective-permute-done.26.refs_2_, ...), custom_call_target="tpu_custom_call", output_to_operand_aliasing={{}: (9, {})} | custom-call | flops 3221225472 | bytes 19922944 | tf_op jit(solution)/shard_map/pallas_call | solution.py:67
  121.8 5.7 %collective-permute-done.8.refs_0_ = f32[128,1024]{1,0:T(8,128)S(1)} collective-permute-done((f32[128,1024]{1,0:T(8,128)S(1)}, f32[128,1024]{1,0:T(8,128)S(1)}, u32[]{:S(2)}, u32[]{:S(2)}) %collective-permute-start.8) | collective-permute-done | bytes 524320 | tf_op jit(solution)/shard_map/ppermute | solution.py:96
  127.5 5.6 %shard_map.30.refs_4_ = f32[2048,1024]{1,0:T(8,128)S(1)} custom-call(s32[2]{0:T(128)S(1)} %pad_add_fusion.flags_ref, f32[128,1024]{1,0:T(8,128)S(1)} %broadcast_select_fusion.3.refs_0_, f32[128,1024]{1,0:T(8,128)S(1)} %broadcast_select_fusion.4.refs_1_, f32[128,1024]{1,0:T(8,128)S(1)} %collective-permute-done.24.refs_2_, ...), custom_call_target="tpu_custom_call", output_to_operand_aliasing={{}: (9, {})} | custom-call | flops 3221225472 | bytes 19922944 | tf_op jit(solution)/shard_map/pallas_call | solution.py:67
  133.1 4.3 %shard_map.31.refs_4_ = f32[2048,1024]{1,0:T(8,128)S(1)} custom-call(s32[2]{0:T(128)S(1)} %pad_add_fusion.flags_ref, f32[128,1024]{1,0:T(8,128)S(1)} %broadcast_select_fusion.2.refs_0_, f32[128,1024]{1,0:T(8,128)S(1)} %collective-permute-done.22.refs_1_, f32[192,1024]{1,0:T(8,128)S(1)} %pad_maximum_fusion.refs_4_.refs_2_, ...), custom_call_target="tpu_custom_call", output_to_operand_aliasing={{}: (5, {})} | custom-call | flops 1610612736 | bytes 18350080 | tf_op jit(solution)/shard_map/pallas_call | solution.py:67
  137.4 3.5 %shard_map.32.refs_5_ = f32[2048,1024]{1,0:T(8,128)} custom-call(s32[2]{0:T(128)S(1)} %pad_add_fusion.flags_ref, f32[128,1024]{1,0:T(8,128)S(1)} %collective-permute-done.8.refs_0_, f32[128,1024]{1,0:T(8,128)S(1)} %collective-permute-done.6.refs_1_, f32[192,1024]{1,0:T(8,128)S(1)} %collective-permute-done.14.refs_6_.refs_2_, ...), custom_call_target="tpu_custom_call" | custom-call | flops 805306368 | bytes 9961472 | tf_op jit(solution)/shard_map/pallas_call | solution.py:67
  141.0 3.5 %shard_map.33 = f32[2048,1024]{1,0:T(8,128)} custom-call(s32[2]{0:T(128)S(1)} %pad_add_fusion.flags_ref, f32[128,1024]{1,0:T(8,128)S(1)} %collective-permute-done.9.refs_0_, f32[128,1024]{1,0:T(8,128)S(1)} %collective-permute-done.10.refs_1_, f32[192,1024]{1,0:T(8,128)S(1)} %collective-permute-done.14.refs_6_.refs_2_, ...), custom_call_target="tpu_custom_call", output_to_operand_aliasing={{}: (6, {})} | custom-call | flops 805306368 | bytes 9961472 | tf_op jit(solution)/shard_map/pallas_call | solution.py:67
  (38 shorter events, 1.7 us)
Async XLA Ops:
  1.1 1.7 %collective-permute-start.1 = (f32[64,1024]{1,0:T(8,128)S(1)}, f32[64,1024]{1,0:T(8,128)S(1)}, u32[]{:S(2)}, u32[]{:S(2)}) collective-permute-start(f32[64,1024]{1,0:T(8,128)S(1)} %get-tuple-element.17), channel_id=1, source_target_pairs={{0,4},{4,0},{1,5},{5,1},{2,6},{6,2},{3,7},{7,3},{8,12},{12,8},{9,1... | collective-permute-start | bytes 786440 | tf_op jit(solution)/shard_map/ppermute | solution.py:94
  1.6 1.5 %collective-permute-start = (f32[64,1024]{1,0:T(8,128)S(1)}, f32[64,1024]{1,0:T(8,128)S(1)}, u32[]{:S(2)}, u32[]{:S(2)}) collective-permute-start(f32[64,1024]{1,0:T(8,128)S(1)} %get-tuple-element.18), channel_id=1, source_target_pairs={{0,4},{4,0},{1,5},{5,1},{2,6},{6,2},{3,7},{7,3},{8,12},{12,8},{9,1... | collective-permute-start | bytes 786440 | tf_op jit(solution)/shard_map/ppermute | solution.py:94
  4.5 10.1 %collective-permute-start.16 = (f32[64,1024]{1,0:T(8,128)S(1)}, f32[64,1024]{1,0:T(8,128)S(1)}, u32[]{:S(2)}, u32[]{:S(2)}) collective-permute-start(f32[64,1024]{1,0:T(8,128)S(1)} %get-tuple-element.10), channel_id=1, source_target_pairs={{0,8},{8,0},{16,24},{24,16},{1,9},{9,1},{17,25},{25,17},{2,10},{10... | collective-permute-start | bytes 786440 | tf_op jit(solution)/shard_map/ppermute | solution.py:95
  7.4 19.2 %collective-permute-start.3 = (f32[64,1024]{1,0:T(8,128)S(1)}, f32[64,1024]{1,0:T(8,128)S(1)}, u32[]{:S(2)}, u32[]{:S(2)}) collective-permute-start(f32[64,1024]{1,0:T(8,128)S(1)} %get-tuple-element.11), channel_id=1, source_target_pairs={{0,24},{8,16},{16,8},{24,0},{1,25},{9,17},{17,9},{25,1},{2,26},{10... | collective-permute-start | bytes 786440 | tf_op jit(solution)/shard_map/ppermute | solution.py:95
  8.9 17.7 %collective-permute-start.2 = (f32[64,1024]{1,0:T(8,128)S(1)}, f32[64,1024]{1,0:T(8,128)S(1)}, u32[]{:S(2)}, u32[]{:S(2)}) collective-permute-start(f32[64,1024]{1,0:T(8,128)S(1)} %get-tuple-element.12), channel_id=1, source_target_pairs={{0,16},{8,24},{16,0},{24,8},{1,17},{9,25},{17,1},{25,9},{2,18},{10... | collective-permute-start | bytes 786440 | tf_op jit(solution)/shard_map/ppermute | solution.py:95
  14.6 46.8 %collective-permute-start.19 = (f32[128,1024]{1,0:T(8,128)S(1)}, f32[128,1024]{1,0:T(8,128)S(1)}, u32[]{:S(2)}, u32[]{:S(2)}) collective-permute-start(f32[128,1024]{1,0:T(8,128)S(1)} %pad_maximum_fusion.1.refs_0_), channel_id=1, source_target_pairs={{0,1},{1,2},{2,3},{4,5},{5,6},{6,7},{8,9},{9,10},{10,11},{12,13},{... | collective-permute-start | bytes 1572872 | tf_op jit(solution)/shard_map/ppermute | solution.py:96
  18.7 43.4 %collective-permute-start.17 = (f32[128,1024]{1,0:T(8,128)S(1)}, f32[128,1024]{1,0:T(8,128)S(1)}, u32[]{:S(2)}, u32[]{:S(2)}) collective-permute-start(f32[128,1024]{1,0:T(8,128)S(1)} %pad_maximum_fusion.1.refs_0_), channel_id=1, source_target_pairs={{1,0},{2,1},{3,2},{5,4},{6,5},{7,6},{9,8},{10,9},{11,10},{13,12},{... | collective-permute-start | bytes 1572872 | tf_op jit(solution)/shard_map/ppermute | solution.py:96
  22.0 20.7 %collective-permute-start.12 = (f32[64,1024]{1,0:T(8,128)S(1)}, f32[64,1024]{1,0:T(8,128)}, u32[]{:S(2)}, u32[]{:S(2)}) collective-permute-start(f32[64,1024]{1,0:T(8,128)S(1)} %get-tuple-element.14), channel_id=1, source_target_pairs={{1,0},{2,1},{3,2},{0,3},{5,4},{6,5},{7,6},{4,7},{9,8},{10,9},{11,1... | collective-permute-start | bytes 786440 | tf_op jit(solution)/shard_map/ppermute | solution.py:96
  26.6 28.1 %collective-permute-start.11 = (f32[64,1024]{1,0:T(8,128)S(1)}, f32[64,1024]{1,0:T(8,128)}, u32[]{:S(2)}, u32[]{:S(2)}) collective-permute-start(f32[64,1024]{1,0:T(8,128)S(1)} %get-tuple-element.15), channel_id=1, source_target_pairs={{3,0},{0,1},{1,2},{2,3},{7,4},{4,5},{5,6},{6,7},{11,8},{8,9},{9,10... | collective-permute-start | bytes 786440 | tf_op jit(solution)/shard_map/ppermute | solution.py:96
  26.6 32.3 %collective-permute-start.13 = (f32[64,1024]{1,0:T(8,128)}, f32[64,1024]{1,0:T(8,128)}, u32[]{:S(2)}, u32[]{:S(2)}) collective-permute-start(f32[64,1024]{1,0:T(8,128)} %get-tuple-element.16), channel_id=1, source_target_pairs={{2,0},{3,1},{0,2},{1,3},{6,4},{7,5},{4,6},{5,7},{10,8},{11,9},{8,1... | collective-permute-start | bytes 786440 | tf_op jit(solution)/shard_map/ppermute | solution.py:96
  42.7 23.5 %collective-permute-start.6 = (f32[128,1024]{1,0:T(8,128)S(1)}, f32[128,1024]{1,0:T(8,128)S(1)}, u32[]{:S(2)}, u32[]{:S(2)}) collective-permute-start(f32[128,1024]{1,0:T(8,128)S(1)} %constant_dynamic-update-slice_fusion.refs_1_), channel_id=1, source_target_pairs={{0,1},{1,2},{2,3},{4,5},{5,6},{6,7},{8,9},{9,10},{10,11},{12,13},{... | collective-permute-start | bytes 1572872 | tf_op jit(solution)/shard_map/ppermute | solution.py:96
  54.7 16.3 %collective-permute-start.4 = (f32[128,1024]{1,0:T(8,128)S(1)}, f32[128,1024]{1,0:T(8,128)S(1)}, u32[]{:S(2)}, u32[]{:S(2)}) collective-permute-start(f32[128,1024]{1,0:T(8,128)S(1)} %constant_dynamic-update-slice_fusion.refs_1_), channel_id=1, source_target_pairs={{1,0},{2,1},{3,2},{5,4},{6,5},{7,6},{9,8},{10,9},{11,10},{13,12},{... | collective-permute-start | bytes 1572872 | tf_op jit(solution)/shard_map/ppermute | solution.py:96
  58.9 7.3 %collective-permute-start.32 = (f32[64,1024]{1,0:T(8,128)S(1)}, f32[64,1024]{1,0:T(8,128)S(1)}, u32[]{:S(2)}, u32[]{:S(2)}) collective-permute-start(f32[64,1024]{1,0:T(8,128)S(1)} %get-tuple-element.13.refs_4_), channel_id=1, source_target_pairs={{0,24},{8,16},{16,8},{24,0},{1,25},{9,17},{17,9},{25,1},{2,26},{10... | collective-permute-start | bytes 786440 | tf_op jit(solution)/shard_map/ppermute | solution.py:95
  61.4 10.4 %collective-permute-start.20 = (f32[128,1024]{1,0:T(8,128)S(1)}, f32[128,1024]{1,0:T(8,128)S(1)}, u32[]{:S(2)}, u32[]{:S(2)}) collective-permute-start(f32[128,1024]{1,0:T(8,128)S(1)} %collective-permute-done.19), channel_id=1, source_target_pairs={{1,2},{2,3},{5,6},{6,7},{9,10},{10,11},{13,14},{14,15},{17,18},{18... | collective-permute-start | bytes 1572872 | tf_op jit(solution)/shard_map/ppermute | solution.py:96
  62.1 14.5 %collective-permute-start.18 = (f32[128,1024]{1,0:T(8,128)S(1)}, f32[128,1024]{1,0:T(8,128)S(1)}, u32[]{:S(2)}, u32[]{:S(2)}) collective-permute-start(f32[128,1024]{1,0:T(8,128)S(1)} %collective-permute-done.17), channel_id=1, source_target_pairs={{1,0},{2,1},{5,4},{6,5},{9,8},{10,9},{13,12},{14,13},{17,16},{18,1... | collective-permute-start | bytes 1572872 | tf_op jit(solution)/shard_map/ppermute | solution.py:96
  66.2 20.6 %collective-permute-start.29 = (f32[128,1024]{1,0:T(8,128)S(1)}, f32[128,1024]{1,0:T(8,128)S(1)}, u32[]{:S(2)}, u32[]{:S(2)}) collective-permute-start(f32[128,1024]{1,0:T(8,128)S(1)} %constant_dynamic-update-slice_fusion.refs_1_), channel_id=1, source_target_pairs={{0,4},{4,0},{1,5},{5,1},{2,6},{6,2},{3,7},{7,3},{8,12},{12,8},{9,1... | collective-permute-start | bytes 1572872 | tf_op jit(solution)/shard_map/ppermute | solution.py:94
  66.2 21.6 %collective-permute-start.28 = (f32[128,1024]{1,0:T(8,128)S(1)}, f32[128,1024]{1,0:T(8,128)S(1)}, u32[]{:S(2)}, u32[]{:S(2)}) collective-permute-start(f32[128,1024]{1,0:T(8,128)S(1)} %pad_maximum_fusion.1.refs_0_), channel_id=1, source_target_pairs={{0,4},{4,0},{1,5},{5,1},{2,6},{6,2},{3,7},{7,3},{8,12},{12,8},{9,1... | collective-permute-start | bytes 1572872 | tf_op jit(solution)/shard_map/ppermute | solution.py:94
  71.0 18.1 %collective-permute-start.7 = (f32[128,1024]{1,0:T(8,128)S(1)}, f32[128,1024]{1,0:T(8,128)S(1)}, u32[]{:S(2)}, u32[]{:S(2)}) collective-permute-start(f32[128,1024]{1,0:T(8,128)S(1)} %collective-permute-done.6.refs_1_), channel_id=1, source_target_pairs={{1,2},{2,3},{5,6},{6,7},{9,10},{10,11},{13,14},{14,15},{17,18},{18... | collective-permute-start | bytes 1572872 | tf_op jit(solution)/shard_map/ppermute | solution.py:96
  71.8 6.4 %collective-permute-start.31 = (f32[64,1024]{1,0:T(8,128)S(1)}, f32[64,1024]{1,0:T(8,128)S(1)}, u32[]{:S(2)}, u32[]{:S(2)}) collective-permute-start(f32[64,1024]{1,0:T(8,128)S(1)} %get-tuple-element.13.refs_4_), channel_id=1, source_target_pairs={{0,16},{8,24},{16,0},{24,8},{1,17},{9,25},{17,1},{25,9},{2,18},{10... | collective-permute-start | bytes 786440 | tf_op jit(solution)/shard_map/ppermute | solution.py:95
  76.6 9.2 %collective-permute-start.30 = (f32[64,1024]{1,0:T(8,128)S(1)}, f32[64,1024]{1,0:T(8,128)S(1)}, u32[]{:S(2)}, u32[]{:S(2)}) collective-permute-start(f32[64,1024]{1,0:T(8,128)S(1)} %get-tuple-element.13.refs_4_), channel_id=1, source_target_pairs={{0,8},{8,0},{16,24},{24,16},{1,9},{9,1},{17,25},{25,17},{2,10},{10... | collective-permute-start | bytes 786440 | tf_op jit(solution)/shard_map/ppermute | solution.py:95
  78.2 30.3 %collective-permute-start.23 = (f32[192,1024]{1,0:T(8,128)S(1)}, f32[192,1024]{1,0:T(8,128)S(1)}, u32[]{:S(2)}, u32[]{:S(2)}) collective-permute-start(f32[192,1024]{1,0:T(8,128)S(1)} %pad_maximum_fusion.refs_4_.refs_2_), channel_id=1, source_target_pairs={{0,8},{8,0},{16,24},{24,16},{1,9},{9,1},{17,25},{25,17},{2,10},{10... | collective-permute-start | bytes 2359304 | tf_op jit(solution)/shard_map/ppermute | solution.py:95
  85.8 27.4 %collective-permute-start.15 = (f32[192,1024]{1,0:T(8,128)S(1)}, f32[192,1024]{1,0:T(8,128)S(1)}, u32[]{:S(2)}, u32[]{:S(2)}) collective-permute-start(f32[192,1024]{1,0:T(8,128)S(1)} %pad_maximum_fusion.refs_4_.refs_2_), channel_id=1, source_target_pairs={{0,24},{8,16},{16,8},{24,0},{1,25},{9,17},{17,9},{25,1},{2,26},{10... | collective-permute-start | bytes 2359304 | tf_op jit(solution)/shard_map/ppermute | solution.py:95
  86.8 28.6 %collective-permute-start.14 = (f32[192,1024]{1,0:T(8,128)S(1)}, f32[192,1024]{1,0:T(8,128)S(1)}, u32[]{:S(2)}, u32[]{:S(2)}) collective-permute-start(f32[192,1024]{1,0:T(8,128)S(1)} %pad_maximum_fusion.refs_4_.refs_2_), channel_id=1, source_target_pairs={{0,16},{8,24},{16,0},{24,8},{1,17},{9,25},{17,1},{25,9},{2,18},{10... | collective-permute-start | bytes 2359304 | tf_op jit(solution)/shard_map/ppermute | solution.py:95
  87.8 15.0 %collective-permute-start.5 = (f32[128,1024]{1,0:T(8,128)S(1)}, f32[128,1024]{1,0:T(8,128)S(1)}, u32[]{:S(2)}, u32[]{:S(2)}) collective-permute-start(f32[128,1024]{1,0:T(8,128)S(1)} %collective-permute-done.4), channel_id=1, source_target_pairs={{1,0},{2,1},{5,4},{6,5},{9,8},{10,9},{13,12},{14,13},{17,16},{18,1... | collective-permute-start | bytes 1572872 | tf_op jit(solution)/shard_map/ppermute | solution.py:96
  89.1 19.3 %collective-permute-start.21 = (f32[128,1024]{1,0:T(8,128)S(1)}, f32[128,1024]{1,0:T(8,128)S(1)}, u32[]{:S(2)}, u32[]{:S(2)}) collective-permute-start(f32[128,1024]{1,0:T(8,128)S(1)} %broadcast_select_fusion.3.refs_0_), channel_id=1, source_target_pairs={{1,0},{2,3},{5,4},{6,7},{9,8},{10,11},{13,12},{14,15},{17,16},{18,... | collective-permute-start | bytes 1572872 | tf_op jit(solution)/shard_map/ppermute | solution.py:96
  102.8 12.7 %collective-permute-start.27 = (f32[128,1024]{1,0:T(8,128)S(1)}, f32[128,1024]{1,0:T(8,128)S(1)}, u32[]{:S(2)}, u32[]{:S(2)}) collective-permute-start(f32[128,1024]{1,0:T(8,128)S(1)} %broadcast_select_fusion.refs_1_), channel_id=1, source_target_pairs={{0,4},{4,0},{1,5},{5,1},{2,6},{6,2},{3,7},{7,3},{8,12},{12,8},{9,1... | collective-permute-start | bytes 1572872 | tf_op jit(solution)/shard_map/ppermute | solution.py:94
  108.4 7.7 %collective-permute-start.26 = (f32[128,1024]{1,0:T(8,128)S(1)}, f32[128,1024]{1,0:T(8,128)S(1)}, u32[]{:S(2)}, u32[]{:S(2)}) collective-permute-start(f32[128,1024]{1,0:T(8,128)S(1)} %broadcast_select_fusion.1.refs_0_), channel_id=1, source_target_pairs={{0,4},{4,0},{1,5},{5,1},{2,6},{6,2},{3,7},{7,3},{8,12},{12,8},{9,1... | collective-permute-start | bytes 1572872 | tf_op jit(solution)/shard_map/ppermute | solution.py:94
  108.5 19.0 %collective-permute-start.25 = (f32[128,1024]{1,0:T(8,128)S(1)}, f32[128,1024]{1,0:T(8,128)S(1)}, u32[]{:S(2)}, u32[]{:S(2)}) collective-permute-start(f32[128,1024]{1,0:T(8,128)S(1)} %broadcast_select_fusion.4.refs_1_), channel_id=1, source_target_pairs={{0,4},{4,0},{1,5},{5,1},{2,6},{6,2},{3,7},{7,3},{8,12},{12,8},{9,1... | collective-permute-start | bytes 1572872 | tf_op jit(solution)/shard_map/ppermute | solution.py:94
  113.2 14.3 %collective-permute-start.8 = (f32[128,1024]{1,0:T(8,128)S(1)}, f32[128,1024]{1,0:T(8,128)S(1)}, u32[]{:S(2)}, u32[]{:S(2)}) collective-permute-start(f32[128,1024]{1,0:T(8,128)S(1)} %broadcast_select_fusion.4.refs_1_), channel_id=1, source_target_pairs={{1,0},{2,3},{5,4},{6,7},{9,8},{10,11},{13,12},{14,15},{17,16},{18,... | collective-permute-start | bytes 1572872 | tf_op jit(solution)/shard_map/ppermute | solution.py:96
  115.4 12.1 %collective-permute-start.24 = (f32[128,1024]{1,0:T(8,128)S(1)}, f32[128,1024]{1,0:T(8,128)S(1)}, u32[]{:S(2)}, u32[]{:S(2)}) collective-permute-start(f32[128,1024]{1,0:T(8,128)S(1)} %broadcast_select_fusion.3.refs_0_), channel_id=1, source_target_pairs={{0,4},{4,0},{1,5},{5,1},{2,6},{6,2},{3,7},{7,3},{8,12},{12,8},{9,1... | collective-permute-start | bytes 1572872 | tf_op jit(solution)/shard_map/ppermute | solution.py:94
  115.5 25.4 %collective-permute-start.10 = (f32[128,1024]{1,0:T(8,128)S(1)}, f32[128,1024]{1,0:T(8,128)S(1)}, u32[]{:S(2)}, u32[]{:S(2)}) collective-permute-start(f32[128,1024]{1,0:T(8,128)S(1)} %collective-permute-done.6.refs_1_), channel_id=1, source_target_pairs={{0,4},{4,0},{1,5},{5,1},{2,6},{6,2},{3,7},{7,3},{8,12},{12,8},{9,1... | collective-permute-start | bytes 1572872 | tf_op jit(solution)/shard_map/ppermute | solution.py:94
  116.1 17.0 %collective-permute-start.22 = (f32[128,1024]{1,0:T(8,128)S(1)}, f32[128,1024]{1,0:T(8,128)S(1)}, u32[]{:S(2)}, u32[]{:S(2)}) collective-permute-start(f32[128,1024]{1,0:T(8,128)S(1)} %broadcast_select_fusion.2.refs_0_), channel_id=1, source_target_pairs={{0,4},{4,0},{1,5},{5,1},{2,6},{6,2},{3,7},{7,3},{8,12},{12,8},{9,1... | collective-permute-start | bytes 1572872 | tf_op jit(solution)/shard_map/ppermute | solution.py:94
  127.5 13.5 %collective-permute-start.9 = (f32[128,1024]{1,0:T(8,128)S(1)}, f32[128,1024]{1,0:T(8,128)S(1)}, u32[]{:S(2)}, u32[]{:S(2)}) collective-permute-start(f32[128,1024]{1,0:T(8,128)S(1)} %collective-permute-done.8.refs_0_), channel_id=1, source_target_pairs={{0,4},{4,0},{1,5},{5,1},{2,6},{6,2},{3,7},{7,3},{8,12},{12,8},{9,1... | collective-permute-start | bytes 1572872 | tf_op jit(solution)/shard_map/ppermute | solution.py:94
